TPU v7x, 32 devices: a whole 2x2x4 slice. The times are simulated.
32 devices in a mesh: dom: 16 (over z, y, x), fault: 2 (over core).
Axes of the slice: x: 2, y: 2, z: 4, core: 2. Of those that a mesh axis runs over, the one named last changes fastest.
Arguments:
- modal_dofs: float32 [9, 56, 4096], P(None, None, ('dom', 'fault')), may hold values from -6 to 6
- star_matrices: float32 [3, 9, 9, 4096], P(None, None, None, ('dom', 'fault')), may hold values from -3.75 to 3.75
- stiffness: float32 [3, 56, 56], replicated, may hold values from -0.75 to 0.75
- face_proj: float32 [4, 56, 21], replicated, may hold values from -0.75 to 0.75
- face_flux: float32 [2, 4, 9, 9, 4096], P(None, None, None, None, ('dom', 'fault')), may hold values from -2 to 2
- neighbour_index: int32 [4, 4096], P(None, ('dom', 'fault')), may hold values from 0 to 767, as said below
- send_faces: int32 [4, 2048], P(None, ('dom', 'fault')), may hold values from 0 to 511, as said below
- fault_faces: int32 [12288], P(('dom', 'fault')), may hold values from 0 to 511, as said below
- fault_count: int32 [16], P('dom'), may hold values from 1 to 384, as said below
- fault_params: float32 [7, 21, 6144], P(None, None, 'dom'), may hold values from 0.03 to 6, as said below
- slip_guess: float32 [21, 6144], P(None, 'dom'), may hold values from 0.1 to 3
- fault_rotation: float32 [6, 9, 6144], P(None, None, 'dom'), may hold values from -2 to 2
- fault_flux: float32 [9, 6, 12288], P(None, None, ('dom', 'fault')), may hold values from -2.5 to 2.5
Outputs:
- new_dofs: float32 [9, 56, 4096], P(None, None, ('dom', 'fault'))
- slip_rate: float32 [21, 12288], P(None, ('dom', 'fault'))
- next_step: float32 [], replicated
Inputs may be any that keep to these rules, and one draw needn't show every extreme that they name: `neighbour_index`: flat faces f * 128 + e of the partition. A value below 512 names a face of the same partition; a value v from 512 on names slot v - 512 of the received blocks in order of o, is carried by a face of an element below 64, and no slot is named twice in a partition. In every draw some partition names all 64 slots of some block. `send_faces`: flat faces of elements below 64 of the sending partition, all different within a partition. `fault_faces`: flat faces of the partition, all different within a partition. `fault_count`: the live slots of a chip are its first ones on both of its partitions; some chip has exactly 384. `fault_params`: Rows: a, state, normal_pre, shear_pre, length, zp, zs; all positive.
All inputs are finite; a program needn't handle non-finite values.
Results may differ from a plain program's by a relative error of at most 0.0003.
Values sent between devices are 32-bit elements; how exact they have to be, the bound alone decides.
A program may use at most 64 MiB of HBM per device.

v0:
```python
import functools

import jax
import jax.numpy as jnp
from jax import lax
from jax.experimental import pallas as pl
from jax.experimental.pallas import tpu as pltpu
from jax.sharding import PartitionSpec as P

DERIVS = 6
NEWTON = 4
REACH = 8
DT_STEP = 0.15
FAR_BOUND = 1e30
LANES = 128
VMEM_BYTES = 67043328
MESH = pl.DeviceIdType.MESH
F32 = jnp.float32
BF16 = jnp.bfloat16


def up(size, unit):
    return -(-size // unit) * unit


def dot(left, right):
    return jnp.dot(left, right, preferred_element_type=F32)


def split(values):
    high = values.astype(BF16)
    low = (values - high.astype(F32)).astype(BF16)
    return high, low


def stacked(values):
    high, low = split(values)
    return jnp.concatenate([high, low], axis=0)


def pick(pair, table):
    half = pair.shape[0] // 2
    both = dot(pair, table)
    return both[:half] + both[half:]


def wide(matrix, width):
    high = matrix.astype(BF16).astype(F32)
    turned = high + pltpu.roll(matrix - high, width, 1)
    return jnp.concatenate([turned, high], axis=1)[:, : 3 * width].astype(BF16)


def product(left_pair, right):
    high, low = split(right)
    half = left_pair.shape[0] // 2
    both = dot(left_pair, high)
    return (both[:half] + both[half:]) + dot(left_pair[:half], low)


def kernel(
    chips,
    cores,
    dofs_hbm,
    star_hbm,
    stiff_hbm,
    proj_hbm,
    flux_hbm,
    neigh_hbm,
    send_hbm,
    faces_hbm,
    count_hbm,
    par_hbm,
    guess_hbm,
    rot_hbm,
    fflux_hbm,
    out_ref,
    slip_ref,
    step_ref,
    dofs_ref,
    star_ref,
    stiff_ref,
    proj_ref,
    flux_ref,
    neigh_ref,
    send_ref,
    faces_ref,
    par_ref,
    guess_ref,
    rot_ref,
    fflux_ref,
    count_ref,
    load_sem,
    x_buf,
    z_buf,
    integ,
    trace,
    pads,
    rows_buf,
    small,
    own_c,
    other_c,
    frame,
    halo_out,
    halo_in,
    lifted,
    fvals,
    bound_out,
    bound_in,
    send_sem,
    recv_sem,
    fault_send,
    fault_recv,
    bound_send,
    bound_recv,
):
    quants, basis, elems = dofs_ref.shape
    points, faces, _ = proj_ref.shape
    slots = faces_ref.shape[0]
    blocks, block = send_ref.shape
    rows = up(points, 8)
    face_rows = LANES // faces
    deep = up(basis, 16)
    flat = faces * elems
    dom = lax.axis_index("dom")
    core = lax.axis_index("fault")
    total = chips * cores
    me = dom * cores + core
    shifts = (1, -1, REACH, -REACH)

    def device_at(shift):
        at = lax.rem(me + shift + total, total)
        return (at // cores, lax.rem(at, cores))

    def chip_at(shift):
        return (lax.rem(dom + shift, chips), core)

    partner = (dom, core + 1 - 2 * lax.rem(core, 2))

    loads = []
    for source, target in (
        (stiff_hbm, stiff_ref),
        (proj_hbm, proj_ref),
        (dofs_hbm, dofs_ref),
        (star_hbm, star_ref),
        (faces_hbm, faces_ref),
        (rot_hbm, rot_ref),
        (par_hbm, par_ref),
        (send_hbm, send_ref),
        (guess_hbm, guess_ref),
        (fflux_hbm, fflux_ref),
        (neigh_hbm, neigh_ref),
        (flux_hbm, flux_ref),
        (count_hbm, count_ref),
    ):
        loads.append(pltpu.make_async_copy(source, target, load_sem.at[len(loads)]))
        loads[-1].start()

    barrier = pltpu.get_barrier_semaphore()
    for shift in shifts:
        pl.semaphore_signal(barrier, inc=1, device_id=device_at(-shift), device_id_type=MESH)
    pl.semaphore_signal(barrier, inc=1, device_id=partner, device_id_type=MESH)

    def greet(hop, carry):
        pl.semaphore_signal(barrier, inc=1, device_id=chip_at(hop), device_id_type=MESH)
        return carry

    lax.fori_loop(1, chips, greet, 0)

    pads[...] = jnp.zeros(pads.shape, F32)
    rows_buf[...] = jnp.zeros(rows_buf.shape, F32)
    small[...] = jnp.zeros(small.shape, jnp.int32)
    loads[0].wait()
    for d in range(3):
        pads[d, 0:basis, 0:basis] = stiff_ref[d]
    stiff_wide = wide(-jnp.concatenate([pads[d, 0:deep] for d in range(3)], axis=0), deep)

    gap = jnp.zeros((deep - basis, LANES), F32)
    pairs = [tuple(range(q, min(q + 2, quants))) for q in range(0, quants, 2)]
    triples = [tuple(range(q, min(q + 3, quants))) for q in range(0, quants, 3)]

    def tall(per_q, group):
        joined = jnp.concatenate(
            [jnp.concatenate([per_q(q), gap], axis=0) for q in group], axis=1
        )
        high, low = split(joined)
        return jnp.concatenate([high, high, low], axis=0)

    def multiply(matrix, per_q, keep):
        for group in pairs:
            result = dot(matrix, tall(per_q, group))
            for n, q in enumerate(group):
                keep(q, result[:, n * elems : (n + 1) * elems])

    def keep_z(q, result):
        for d in range(3):
            z_buf[d, q] = result[d * deep : d * deep + basis]

    def apply_star(group):
        sums = [None] * len(group)
        for d in range(3):
            for j in range(quants):
                column = z_buf[d, j]
                for n, q in enumerate(group):
                    term = star_ref[q, j, d : d + 1, :] * column
                    sums[n] = term if sums[n] is None else sums[n] + term
        return sums

    loads[1].wait()
    for p in range(points):
        rows_buf[p * faces : (p + 1) * faces, 0:basis] = proj_ref[p]
    for f in range(faces):
        pads[3, f * face_rows : f * face_rows + rows] = rows_buf[pl.ds(f, rows, faces), :]
    trace_wide = wide(pads[3], deep)
    loads[2].wait()
    loads[3].wait()
    factor = DT_STEP
    for degree in range(1, DERIVS):
        if degree == 1:
            multiply(stiff_wide, lambda q: dofs_ref[q], keep_z)
        else:
            multiply(stiff_wide, lambda q: x_buf[q], keep_z)
        past = factor
        factor = factor * DT_STEP / (degree + 1)
        for group in triples:
            for q, fresh in zip(group, apply_star(group)):
                if degree < DERIVS - 1:
                    x_buf[q] = fresh
                base = past * dofs_ref[q] if degree == 1 else integ[q]
                integ[q] = base + factor * fresh

    for k in (4, 5, 6):
        loads[k].wait()
    trace[quants * rows :, :] = jnp.zeros((trace.shape[0] - quants * rows, flat), F32)

    def keep_trace(q, result):
        for f in range(faces):
            first = f * face_rows
            trace[q * rows : (q + 1) * rows, f * elems : (f + 1) * elems] = result[
                first : first + rows
            ]

    multiply(trace_wide, lambda q: integ[q], keep_trace)
    trace_split = stacked(trace[...])

    def table(keys, wanted):
        return jnp.where(keys == wanted, 1.0, 0.0).astype(BF16)

    fault_keys = lax.broadcasted_iota(jnp.int32, (flat, slots), 0)
    fault_table = table(fault_keys, faces_ref[...].reshape(1, slots))
    own_trace = pick(trace_split, fault_table)
    orient = jnp.where(core == 0, 1.0, -1.0).astype(F32)
    for k in range(6):
        summed = None
        for j in range(quants):
            term = rot_ref[j, k : k + 1, :] * own_trace[j * rows : (j + 1) * rows]
            summed = term if summed is None else summed + term
        frame[k] = summed
    for k in range(3):
        impedance = par_ref[5 if k == 0 else 6]
        own_c[k, 0:points] = frame[k, 0:points] - orient * impedance * frame[k + 3, 0:points]

    pl.semaphore_wait(barrier, len(shifts) + chips)
    to_partner = pltpu.make_async_remote_copy(
        src_ref=own_c,
        dst_ref=other_c,
        send_sem=fault_send,
        recv_sem=fault_recv,
        device_id=partner,
        device_id_type=MESH,
    )
    to_partner.start()

    loads[7].wait()
    small[0:blocks, 0:block] = send_ref[...]
    half_rows = trace.shape[0] // 2
    doubled = small[...] + pltpu.roll(small[...], block, 1)
    lane = lax.broadcasted_iota(jnp.int32, (half_rows, LANES), 1)
    block_keys = lax.broadcasted_iota(jnp.int32, (flat, blocks * LANES), 0)
    wanted = jnp.concatenate([doubled[o : o + 1] for o in range(blocks)], axis=1)
    chosen = pick(trace_split, table(block_keys, wanted))
    copies = []
    for o, shift in enumerate(shifts):
        part = chosen[:, o * LANES : (o + 1) * LANES]
        halo_out[o] = jnp.where(lane < block, part[:half_rows], part[half_rows:])
        copies.append(
            pltpu.make_async_remote_copy(
                src_ref=halo_out.at[o],
                dst_ref=halo_in.at[o],
                send_sem=send_sem.at[o],
                recv_sem=recv_sem.at[o],
                device_id=device_at(shift),
                device_id_type=MESH,
            )
        )
        copies[-1].start()

    loads[8].wait()
    loads[12].wait()
    to_partner.wait()
    fric_a, state_value, normal_pre, shear_pre = (par_ref[k] for k in range(4))
    imp_p, imp_s = par_ref[5], par_ref[6]
    normal_hat = 0.5 * (own_c[0, 0:points] + other_c[0, 0:points])
    locked = shear_pre + 0.5 * (own_c[1, 0:points] + other_c[1, 0:points])
    dip_hat = 0.5 * (own_c[2, 0:points] + other_c[2, 0:points])
    effective = jnp.maximum(normal_pre - normal_hat, 0.0)
    growth = 0.5 * jnp.exp(state_value / fric_a)
    strength = effective * fric_a
    slip_speed = guess_ref[...]
    for _ in range(NEWTON):
        scaled = slip_speed * growth
        magnitude = jnp.abs(scaled)
        root = jnp.sqrt(1.0 + scaled * scaled)
        logged = jnp.log(magnitude + root)
        logged = jnp.where(scaled < 0.0, -logged, logged)
        mismatch = locked - 0.5 * imp_s * slip_speed - strength * logged
        slope_value = -0.5 * imp_s - strength * growth / root
        slip_speed = slip_speed - mismatch / slope_value
    shear_hat = locked - shear_pre - 0.5 * imp_s * slip_speed
    live = lax.broadcasted_iota(jnp.int32, (points, slots), 1) < count_ref[0]
    slip_ref[...] = jnp.where(live, slip_speed, 0.0)
    bound = jnp.where(live, par_ref[4] / (jnp.abs(slip_speed) + 1.0), FAR_BOUND)
    bound = jnp.min(jnp.min(bound, axis=0, keepdims=True), axis=1, keepdims=True)
    best = jnp.broadcast_to(bound, (8, LANES))
    bound_out[...] = best

    def bound_copy(hop):
        return pltpu.make_async_remote_copy(
            src_ref=bound_out,
            dst_ref=bound_in.at[hop - 1],
            send_sem=bound_send.at[hop - 1],
            recv_sem=bound_recv.at[hop - 1],
            device_id=chip_at(hop),
            device_id_type=MESH,
        )

    def send_bound(hop, carry):
        bound_copy(hop).start()
        return carry

    lax.fori_loop(1, chips, send_bound, 0)

    turned = [jnp.transpose(pads[d])[0:deep] for d in range(3)]
    turned_wide = wide(jnp.concatenate(turned, axis=0), deep)
    multiply(turned_wide, lambda q: integ[q], keep_z)
    for group in triples:
        for q, fresh in zip(group, apply_star(group)):
            out_ref[q] = dofs_ref[q] + fresh

    loads[9].wait()
    hats = [normal_hat, shear_hat, dip_hat]
    for k in range(3):
        impedance = imp_p if k == 0 else imp_s
        hats.append(
            frame[k + 3, 0:points] + orient * (hats[k] - frame[k, 0:points]) / impedance
        )
    fvals[...] = jnp.zeros(fvals.shape, F32)
    for q in range(quants):
        summed = None
        for k in range(6):
            term = fflux_ref[q, k : k + 1, :] * hats[k]
            summed = term if summed is None else summed + term
        fvals[q * rows : q * rows + points, :] = jnp.where(live, summed, 0.0)
    spread_pair = stacked(fvals[...])
    spread = lax.dot_general(
        spread_pair, fault_table, (((1,), (1,)), ((), ())), preferred_element_type=F32
    )
    half = spread.shape[0] // 2
    lifted[...] = spread[:half] + spread[half:]

    loads[10].wait()
    loads[11].wait()
    neighbour = jnp.concatenate([neigh_ref[f : f + 1, :] for f in range(faces)], axis=1)
    face_keys = lax.broadcasted_iota(jnp.int32, (flat, flat), 0)
    local_part = pick(trace_split, table(face_keys, neighbour))
    place = lax.broadcasted_iota(jnp.int32, (blocks * LANES, flat), 0)
    spot = lax.rem(place, LANES)
    slot_key = flat + place // LANES * block
    top_table = table(jnp.where(spot < block, slot_key + spot, -1), neighbour)
    low_table = table(jnp.where(spot < block, -1, slot_key + spot - block), neighbour)

    for copy in copies:
        copy.wait()
    arrived = stacked(jnp.concatenate([halo_in[o] for o in range(blocks)], axis=1))
    outer = local_part + jnp.concatenate(
        [pick(arrived, top_table), pick(arrived, low_table)], axis=0
    )
    lift_pair = stacked(jnp.transpose(pads[3])[:deep])
    pieces = []
    for f in range(faces):
        columns = slice(f * elems, (f + 1) * elems)
        values = []
        for q in range(quants):
            summed = lifted[q * rows : (q + 1) * rows, columns]
            for j in range(quants):
                inner = trace[j * rows : (j + 1) * rows, columns]
                near = outer[j * rows : (j + 1) * rows, columns]
                summed = summed + flux_ref[0, q, j, f : f + 1, :] * inner
                summed = summed + flux_ref[1, q, j, f : f + 1, :] * near
            values.append(summed)
        pieces.append(values)
    rest = jnp.zeros((face_rows - rows, LANES), F32)
    for group in pairs:
        columns = [
            jnp.concatenate(
                [part for f in range(faces) for part in (pieces[f][q], rest)], axis=0
            )
            for q in group
        ]
        result = product(lift_pair, jnp.concatenate(columns, axis=1))[:basis]
        for n, q in enumerate(group):
            out_ref[q] = out_ref[q] - result[:, n * elems : (n + 1) * elems]

    def end_bound(hop, carry):
        bound_copy(hop).wait()
        return carry

    lax.fori_loop(1, chips, end_bound, 0)
    if chips > 1:
        best = jnp.minimum(bound_out[...], jnp.min(bound_in[...], axis=0))
    step_ref[...] = best[0:1, 0:1]


def store(dofs, slip, step, dofs_out, slip_out, step_out, sems):
    moves = ((dofs, dofs_out), (slip, slip_out), (step, step_out))
    copies = [pltpu.make_async_copy(a, b, sems.at[n]) for n, (a, b) in enumerate(moves)]
    for copy in copies:
        copy.start()
    for copy in copies:
        copy.wait()


def solution(mesh):
    chips, cores = mesh.shape["dom"], mesh.shape["fault"]
    hops = max(1, chips - 1)

    def on_device(
        modal_dofs,
        star_matrices,
        stiffness,
        face_proj,
        face_flux,
        neighbour_index,
        send_faces,
        fault_faces,
        fault_count,
        fault_params,
        slip_guess,
        fault_rotation,
        fault_flux,
    ):
        quants, basis, elems = modal_dofs.shape
        faces, _, points = face_proj.shape
        slots = fault_faces.shape[0]
        blocks = send_faces.shape[0]
        rows = up(points, 8)
        trace_rows = up(quants * rows, 32)
        star_matrices = jnp.transpose(star_matrices, (1, 2, 0, 3))
        face_proj = jnp.transpose(face_proj, (2, 0, 1))
        face_flux = jnp.transpose(face_flux, (0, 2, 3, 1, 4))
        fault_rotation = jnp.transpose(fault_rotation, (1, 0, 2))
        loaded = (
            modal_dofs,
            star_matrices,
            stiffness,
            face_proj,
            face_flux,
            neighbour_index,
            send_faces,
            fault_faces,
            fault_params,
            slip_guess,
            fault_rotation,
            fault_flux,
        )
        held = 4 * (quants * up(basis, 8) * elems + (rows + 8) * slots)
        vmem = pl.BlockSpec(memory_space=pltpu.VMEM)
        hbm = pl.BlockSpec(memory_space=pl.ANY)
        new_dofs, slip_rate, next_step = pl.pallas_call(
            functools.partial(kernel, chips, cores),
            out_shape=(
                pltpu.VMEM(modal_dofs.shape, F32),
                pltpu.VMEM(slip_guess.shape, F32),
                pltpu.VMEM((1, 1), F32),
            ),
            in_specs=[hbm] * 13,
            out_specs=(vmem, vmem, vmem),
            scratch_shapes=[
                *(pltpu.VMEM(array.shape, array.dtype) for array in loaded),
                pltpu.SMEM(fault_count.shape, fault_count.dtype),
                pltpu.SemaphoreType.DMA((len(loaded) + 1,)),
                pltpu.VMEM((quants, basis, elems), F32),
                pltpu.VMEM((3, quants, basis, elems), F32),
                pltpu.VMEM((quants, basis, elems), F32),
                pltpu.VMEM((trace_rows, faces * elems), F32),
                pltpu.VMEM((4, LANES, LANES), F32),
                pltpu.VMEM((up(rows * faces, 8), LANES), F32),
                pltpu.VMEM((up(blocks, 8), LANES), jnp.int32),
                pltpu.VMEM((3, points, slots), F32),
                pltpu.VMEM((3, points, slots), F32),
                pltpu.VMEM((6, rows, slots), F32),
                pltpu.VMEM((blocks, trace_rows // 2, LANES), F32),
                pltpu.VMEM((blocks, trace_rows // 2, LANES), F32),
                pltpu.VMEM((trace_rows, faces * elems), F32),
                pltpu.VMEM((trace_rows, slots), F32),
                pltpu.VMEM((8, LANES), F32),
                pltpu.VMEM((hops, 8, LANES), F32),
                pltpu.SemaphoreType.DMA((blocks,)),
                pltpu.SemaphoreType.DMA((blocks,)),
                pltpu.SemaphoreType.DMA,
                pltpu.SemaphoreType.DMA,
                pltpu.SemaphoreType.DMA((hops,)),
                pltpu.SemaphoreType.DMA((hops,)),
            ],
            compiler_params=pltpu.CompilerParams(
                collective_id=0, has_side_effects=True, vmem_limit_bytes=VMEM_BYTES - held
            ),
        )(
            modal_dofs,
            star_matrices,
            stiffness,
            face_proj,
            face_flux,
            neighbour_index,
            send_faces,
            fault_faces,
            fault_count,
            fault_params,
            slip_guess,
            fault_rotation,
            fault_flux,
        )
        results = (new_dofs, slip_rate, next_step)
        new_dofs, slip_rate, next_step = pl.pallas_call(
            store,
            out_shape=tuple(jax.ShapeDtypeStruct(r.shape, r.dtype) for r in results),
            in_specs=[vmem] * len(results),
            out_specs=(hbm,) * len(results),
            scratch_shapes=[pltpu.SemaphoreType.DMA((len(results),))],
            compiler_params=pltpu.CompilerParams(vmem_limit_bytes=4 * 1024 * 1024),
        )(*results)
        return new_dofs, slip_rate, next_step.reshape(())

    return jax.shard_map(
        on_device,
        mesh=mesh,
        in_specs=(
            P(None, None, ("dom", "fault")),
            P(None, None, None, ("dom", "fault")),
            P(),
            P(),
            P(None, None, None, None, ("dom", "fault")),
            P(None, ("dom", "fault")),
            P(None, ("dom", "fault")),
            P(("dom", "fault")),
            P("dom"),
            P(None, None, "dom"),
            P(None, "dom"),
            P(None, None, "dom"),
            P(None, None, ("dom", "fault")),
        ),
        out_specs=(P(None, None, ("dom", "fault")), P(None, ("dom", "fault")), P()),
        check_vma=False,
    )
```

profile of v0, /device:TPU:0, one launch (start us, length us, event | category | flops | bytes accessed | tf_op | source)
XLA Modules:
  0.0 20.4 jit_solution(475253607817132649)
XLA Ops:
  1.3 17.8 %shard_map.148 = (f32[9,56,128]{2,1,0:T(8,128)S(1)}, f32[21,384]{1,0:T(8,128)S(1)}, f32[1,1]{1,0:T(1,128)}) custom-call(f32[9,56,128]{2,1,0:T(8,128)} %dofs_hbm.1, f32[9,9,3,128]{3,2,1,0:T(4,128)} %bitcast.6, f32[3,56,56]{2,1,0:T(8,128)} %stiff_hbm.1, f32[21,4,56]{2,1,0:T(4,128)} %bitcast.8, f32[2,9,9,4,128]{4,3,2,1,0:T(4,128)} %bitcast.5, ...), custom_call_target="tpu_custom_call" | custom-call | tf_op jit(solution)/shard_map/pallas_call | solution.py:478
  19.0 1.4 %shard_map.149 = (f32[9,56,128]{2,1,0:T(8,128)}, f32[21,384]{1,0:T(8,128)}, f32[1,1]{1,0:T(1,128)}) custom-call(f32[9,56,128]{2,1,0:T(8,128)S(1)} %get-tuple-element.9.dofs, f32[21,384]{1,0:T(8,128)S(1)} %get-tuple-element.10.slip, f32[1,1]{1,0:T(1,128)} %get-tuple-element.11.step), custom_call_target="tpu_custom_call" | custom-call | tf_op jit(solution)/shard_map/pallas_call | solution.py:533
where the time goes:
time: 20.6 us; the launch traced here: 20.4 us
  Pallas kernels  19.1 us (93%)
  between operations  1.29 us (6%)
    pallas_call x1, Pallas kernels, on_device(): pl.pallas_call(functools.partial(kernel, chips, cores), out_shape=(pltpu....  17.8 us
    pallas_call x1, Pallas kernels, on_device(): pl.pallas_call(store, out_shape=tuple((jax.ShapeDtypeStruct(r.shape, r.dt...  1.36 us

commit v1 on v0

--- a/solution.py
+++ b/solution.py
@@ -153,18 +153,25 @@
         (count_hbm, count_ref),
     ):
         loads.append(pltpu.make_async_copy(source, target, load_sem.at[len(loads)]))
-        loads[-1].start()
+    for load in loads[:4]:
+        load.start()
 
     barrier = pltpu.get_barrier_semaphore()
     for shift in shifts:
         pl.semaphore_signal(barrier, inc=1, device_id=device_at(-shift), device_id_type=MESH)
     pl.semaphore_signal(barrier, inc=1, device_id=partner, device_id_type=MESH)
 
-    def greet(hop, carry):
+    def each_hop(step):
+        if chips <= 32:
+            for hop in range(1, chips):
+                step(hop)
+        else:
+            lax.fori_loop(1, chips, lambda hop, carry: (step(hop), carry)[1], 0)
+
+    def greet(hop):
         pl.semaphore_signal(barrier, inc=1, device_id=chip_at(hop), device_id_type=MESH)
-        return carry
-
-    lax.fori_loop(1, chips, greet, 0)
+
+    each_hop(greet)
 
     pads[...] = jnp.zeros(pads.shape, F32)
     rows_buf[...] = jnp.zeros(rows_buf.shape, F32)
@@ -213,6 +220,8 @@
     trace_wide = wide(pads[3], deep)
     loads[2].wait()
     loads[3].wait()
+    for load in loads[4:]:
+        load.start()
     factor = DT_STEP
     for degree in range(1, DERIVS):
         if degree == 1:
@@ -294,9 +303,16 @@
         )
         copies[-1].start()
 
+    turned = [jnp.transpose(pads[d])[0:deep] for d in range(3)]
+    turned_wide = wide(jnp.concatenate(turned, axis=0), deep)
+    multiply(turned_wide, lambda q: integ[q], keep_z)
+    for group in triples:
+        for q, fresh in zip(group, apply_star(group)):
+            out_ref[q] = dofs_ref[q] + fresh
+
     loads[8].wait()
     loads[12].wait()
-    to_partner.wait()
+    to_partner.wait_recv()
     fric_a, state_value, normal_pre, shear_pre = (par_ref[k] for k in range(4))
     imp_p, imp_s = par_ref[5], par_ref[6]
     normal_hat = 0.5 * (own_c[0, 0:points] + other_c[0, 0:points])
@@ -320,31 +336,19 @@
     slip_ref[...] = jnp.where(live, slip_speed, 0.0)
     bound = jnp.where(live, par_ref[4] / (jnp.abs(slip_speed) + 1.0), FAR_BOUND)
     bound = jnp.min(jnp.min(bound, axis=0, keepdims=True), axis=1, keepdims=True)
-    best = jnp.broadcast_to(bound, (8, LANES))
-    bound_out[...] = best
-
-    def bound_copy(hop):
-        return pltpu.make_async_remote_copy(
+    bound_out[...] = jnp.broadcast_to(bound, (1, LANES))
+
+    def send_bound(hop):
+        pltpu.make_async_remote_copy(
             src_ref=bound_out,
             dst_ref=bound_in.at[hop - 1],
-            send_sem=bound_send.at[hop - 1],
-            recv_sem=bound_recv.at[hop - 1],
+            send_sem=bound_send,
+            recv_sem=bound_recv,
             device_id=chip_at(hop),
             device_id_type=MESH,
-        )
-
-    def send_bound(hop, carry):
-        bound_copy(hop).start()
-        return carry
-
-    lax.fori_loop(1, chips, send_bound, 0)
-
-    turned = [jnp.transpose(pads[d])[0:deep] for d in range(3)]
-    turned_wide = wide(jnp.concatenate(turned, axis=0), deep)
-    multiply(turned_wide, lambda q: integ[q], keep_z)
-    for group in triples:
-        for q, fresh in zip(group, apply_star(group)):
-            out_ref[q] = dofs_ref[q] + fresh
+        ).start()
+
+    each_hop(send_bound)
 
     loads[9].wait()
     hats = [normal_hat, shear_hat, dip_hat]
@@ -379,7 +383,7 @@
     low_table = table(jnp.where(spot < block, -1, slot_key + spot - block), neighbour)
 
     for copy in copies:
-        copy.wait()
+        copy.wait_recv()
     arrived = stacked(jnp.concatenate([halo_in[o] for o in range(blocks)], axis=1))
     outer = local_part + jnp.concatenate(
         [pick(arrived, top_table), pick(arrived, low_table)], axis=0
@@ -410,18 +414,20 @@
         for n, q in enumerate(group):
             out_ref[q] = out_ref[q] - result[:, n * elems : (n + 1) * elems]
 
-    def end_bound(hop, carry):
-        bound_copy(hop).wait()
-        return carry
-
-    lax.fori_loop(1, chips, end_bound, 0)
+    to_partner.wait_send()
+    for copy in copies:
+        copy.wait_send()
+    best = bound_out[...]
     if chips > 1:
-        best = jnp.minimum(bound_out[...], jnp.min(bound_in[...], axis=0))
-    step_ref[...] = best[0:1, 0:1]
-
-
-def store(dofs, slip, step, dofs_out, slip_out, step_out, sems):
-    moves = ((dofs, dofs_out), (slip, slip_out), (step, step_out))
+        pltpu.make_async_copy(bound_in, bound_in, bound_send).wait()
+        pltpu.make_async_copy(bound_in, bound_in, bound_recv).wait()
+        best = jnp.minimum(best, jnp.min(bound_in[...], axis=0))
+    step_ref[...] = jnp.broadcast_to(best, step_ref.shape)
+
+
+def store(dofs, slip, step, dofs_out, slip_out, step_out, least, sems):
+    least[...] = step[0:1, 0:1]
+    moves = ((dofs, dofs_out), (slip, slip_out), (least, step_out))
     copies = [pltpu.make_async_copy(a, b, sems.at[n]) for n, (a, b) in enumerate(moves)]
     for copy in copies:
         copy.start()
@@ -480,7 +486,7 @@
             out_shape=(
                 pltpu.VMEM(modal_dofs.shape, F32),
                 pltpu.VMEM(slip_guess.shape, F32),
-                pltpu.VMEM((1, 1), F32),
+                pltpu.VMEM((8, LANES), F32),
             ),
             in_specs=[hbm] * 13,
             out_specs=(vmem, vmem, vmem),
@@ -502,14 +508,14 @@
                 pltpu.VMEM((blocks, trace_rows // 2, LANES), F32),
                 pltpu.VMEM((trace_rows, faces * elems), F32),
                 pltpu.VMEM((trace_rows, slots), F32),
-                pltpu.VMEM((8, LANES), F32),
-                pltpu.VMEM((hops, 8, LANES), F32),
+                pltpu.VMEM((1, LANES), F32),
+                pltpu.VMEM((hops, 1, LANES), F32),
                 pltpu.SemaphoreType.DMA((blocks,)),
                 pltpu.SemaphoreType.DMA((blocks,)),
                 pltpu.SemaphoreType.DMA,
                 pltpu.SemaphoreType.DMA,
-                pltpu.SemaphoreType.DMA((hops,)),
-                pltpu.SemaphoreType.DMA((hops,)),
+                pltpu.SemaphoreType.DMA,
+                pltpu.SemaphoreType.DMA,
             ],
             compiler_params=pltpu.CompilerParams(
                 collective_id=0, has_side_effects=True, vmem_limit_bytes=VMEM_BYTES - held
@@ -532,10 +538,14 @@
         results = (new_dofs, slip_rate, next_step)
         new_dofs, slip_rate, next_step = pl.pallas_call(
             store,
-            out_shape=tuple(jax.ShapeDtypeStruct(r.shape, r.dtype) for r in results),
+            out_shape=(
+                jax.ShapeDtypeStruct(new_dofs.shape, F32),
+                jax.ShapeDtypeStruct(slip_rate.shape, F32),
+                jax.ShapeDtypeStruct((1, 1), F32),
+            ),
             in_specs=[vmem] * len(results),
             out_specs=(hbm,) * len(results),
-            scratch_shapes=[pltpu.SemaphoreType.DMA((len(results),))],
+            scratch_shapes=[pltpu.VMEM((1, 1), F32), pltpu.SemaphoreType.DMA((len(results),))],
             compiler_params=pltpu.CompilerParams(vmem_limit_bytes=4 * 1024 * 1024),
         )(*results)
         return new_dofs, slip_rate, next_step.reshape(())

time: 20.6 us -> 18.9 us (0.917)
  Pallas kernels: 19.1 us -> 17.4 us
    pallas_call x1, Pallas kernels: 17.8 us -> 16.7 us  [on_device(): pl.pallas_call(functools.partial(kernel, chips, cores), out_shape=(pltpu....]
    pallas_call x1, Pallas kernels: 1.36 us -> 0.73 us  [on_device(): pl.pallas_call(store, out_shape=(jax.ShapeDtypeStruct(new_dofs.shape, F32...]
where the time goes in v1:
time: 18.9 us; the launch traced here: 18.7 us
  Pallas kernels  17.4 us (92%)
  between operations  1.29 us (7%)
    pallas_call x1, Pallas kernels, on_device(): pl.pallas_call(functools.partial(kernel, chips, cores), out_shape=(pltpu....  16.7 us
    pallas_call x1, Pallas kernels, on_device(): pl.pallas_call(store, out_shape=(jax.ShapeDtypeStruct(new_dofs.shape, F32...  0.73 us

profile of v1, /device:TPU:0, one launch (start us, length us, event | category | flops | bytes accessed | tf_op | source)
XLA Modules:
  0.0 18.7 jit_solution(6227890051660455877)
XLA Ops:
  1.3 16.7 %shard_map.148 = (f32[9,56,128]{2,1,0:T(8,128)S(1)}, f32[21,384]{1,0:T(8,128)S(1)}, f32[8,128]{1,0:T(8,128)S(1)}) custom-call(f32[9,56,128]{2,1,0:T(8,128)} %dofs_hbm.1, f32[9,9,3,128]{3,2,1,0:T(4,128)} %bitcast.6, f32[3,56,56]{2,1,0:T(8,128)} %stiff_hbm.1, f32[21,4,56]{2,1,0:T(4,128)} %bitcast.8, f32[2,9,9,4,128]{4,3,2,1,0:T(4,128)} %bitcast.5, ...), custom_call_target="tpu_custom_call" | custom-call | tf_op jit(solution)/shard_map/pallas_call | solution.py:484
  18.0 0.7 %shard_map.149 = (f32[9,56,128]{2,1,0:T(8,128)}, f32[21,384]{1,0:T(8,128)}, f32[1,1]{1,0:T(1,128)}) custom-call(f32[9,56,128]{2,1,0:T(8,128)S(1)} %get-tuple-element.9.dofs, f32[21,384]{1,0:T(8,128)S(1)} %get-tuple-element.10.slip, f32[8,128]{1,0:T(8,128)S(1)} %get-tuple-element.11.step), custom_call_target="tpu_custom_call" | custom-call | tf_op jit(solution)/shard_map/pallas_call | solution.py:539

commit v2 on v1

--- a/solution.py
+++ b/solution.py
@@ -13,6 +13,7 @@
 DT_STEP = 0.15
 FAR_BOUND = 1e30
 LANES = 128
+EDGE = 64
 VMEM_BYTES = 67043328
 MESH = pl.DeviceIdType.MESH
 F32 = jnp.float32
@@ -44,17 +45,15 @@
     return both[:half] + both[half:]
 
 
+def pick_apart(pair, table):
+    half = pair.shape[0] // 2
+    return dot(pair[:half], table) + dot(pair[half:], table)
+
+
 def wide(matrix, width):
     high = matrix.astype(BF16).astype(F32)
     turned = high + pltpu.roll(matrix - high, width, 1)
     return jnp.concatenate([turned, high], axis=1)[:, : 3 * width].astype(BF16)
-
-
-def product(left_pair, right):
-    high, low = split(right)
-    half = left_pair.shape[0] // 2
-    both = dot(left_pair, high)
-    return (both[:half] + both[half:]) + dot(left_pair[:half], low)
 
 
 def kernel(
@@ -104,6 +103,8 @@
     halo_in,
     lifted,
     fvals,
+    vals,
+    pair_flux,
     bound_out,
     bound_in,
     send_sem,
@@ -136,25 +137,48 @@
 
     partner = (dom, core + 1 - 2 * lax.rem(core, 2))
 
+    def load(source, target):
+        copy = pltpu.make_async_copy(source, target, load_sem.at[len(loads)])
+        loads.append(copy)
+        return copy
+
     loads = []
-    for source, target in (
-        (stiff_hbm, stiff_ref),
-        (proj_hbm, proj_ref),
-        (dofs_hbm, dofs_ref),
-        (star_hbm, star_ref),
-        (faces_hbm, faces_ref),
-        (rot_hbm, rot_ref),
-        (par_hbm, par_ref),
-        (send_hbm, send_ref),
-        (guess_hbm, guess_ref),
-        (fflux_hbm, fflux_ref),
-        (neigh_hbm, neigh_ref),
-        (flux_hbm, flux_ref),
-        (count_hbm, count_ref),
-    ):
-        loads.append(pltpu.make_async_copy(source, target, load_sem.at[len(loads)]))
-    for load in loads[:4]:
-        load.start()
+    first = [
+        load(source, target)
+        for source, target in (
+            (stiff_hbm, stiff_ref),
+            (proj_hbm, proj_ref),
+            (dofs_hbm, dofs_ref),
+            (star_hbm, star_ref),
+        )
+    ]
+    later = [
+        load(source, target)
+        for source, target in (
+            (faces_hbm, faces_ref),
+            (rot_hbm, rot_ref),
+            *((par_hbm.at[k], par_ref.at[k]) for k in (5, 6)),
+            (send_hbm, send_ref),
+            *((par_hbm.at[k], par_ref.at[k]) for k in range(5)),
+            (guess_hbm, guess_ref),
+            (count_hbm, count_ref),
+            (fflux_hbm, fflux_ref),
+            (neigh_hbm, neigh_ref),
+            (flux_hbm.at[0], flux_ref.at[0]),
+            (flux_hbm.at[1], flux_ref.at[1]),
+        )
+    ]
+    for copy in first:
+        copy.start()
+    waiting = list(later)
+
+    def fence():
+        if waiting:
+            waiting.pop(0).wait()
+
+    def arrived(number):
+        while len(later) - len(waiting) < number:
+            fence()
 
     barrier = pltpu.get_barrier_semaphore()
     for shift in shifts:
@@ -176,13 +200,15 @@
     pads[...] = jnp.zeros(pads.shape, F32)
     rows_buf[...] = jnp.zeros(rows_buf.shape, F32)
     small[...] = jnp.zeros(small.shape, jnp.int32)
-    loads[0].wait()
+    vals[...] = jnp.zeros(vals.shape, F32)
+    first[0].wait()
+    for copy in later:
+        copy.start()
     for d in range(3):
         pads[d, 0:basis, 0:basis] = stiff_ref[d]
     stiff_wide = wide(-jnp.concatenate([pads[d, 0:deep] for d in range(3)], axis=0), deep)
 
     gap = jnp.zeros((deep - basis, LANES), F32)
-    pairs = [tuple(range(q, min(q + 2, quants))) for q in range(0, quants, 2)]
     triples = [tuple(range(q, min(q + 3, quants))) for q in range(0, quants, 3)]
 
     def tall(per_q, group):
@@ -192,70 +218,77 @@
         high, low = split(joined)
         return jnp.concatenate([high, high, low], axis=0)
 
-    def multiply(matrix, per_q, keep):
-        for group in pairs:
-            result = dot(matrix, tall(per_q, group))
-            for n, q in enumerate(group):
-                keep(q, result[:, n * elems : (n + 1) * elems])
-
-    def keep_z(q, result):
-        for d in range(3):
-            z_buf[d, q] = result[d * deep : d * deep + basis]
-
-    def apply_star(group):
+    def multiply(matrix, per_q, keep, group):
+        result = dot(matrix, tall(per_q, group))
+        for n, q in enumerate(group):
+            keep(q, result[:, n * elems : (n + 1) * elems])
+
+    def keep_z(at):
+        def keep(q, result):
+            for d in range(3):
+                z_buf[at, d, q] = result[d * deep : d * deep + basis]
+
+        return keep
+
+    def keep_trace(q, result):
+        for f in range(faces):
+            first_row = f * face_rows
+            trace[q * rows : (q + 1) * rows, f * elems : (f + 1) * elems] = result[
+                first_row : first_row + rows
+            ]
+
+    def apply_star(at, group):
         sums = [None] * len(group)
-        for d in range(3):
-            for j in range(quants):
-                column = z_buf[d, j]
+        for j in range(quants):
+            for d in range(3):
+                column = z_buf[at, d, j]
                 for n, q in enumerate(group):
                     term = star_ref[q, j, d : d + 1, :] * column
                     sums[n] = term if sums[n] is None else sums[n] + term
         return sums
 
-    loads[1].wait()
+    first[1].wait()
     for p in range(points):
         rows_buf[p * faces : (p + 1) * faces, 0:basis] = proj_ref[p]
     for f in range(faces):
         pads[3, f * face_rows : f * face_rows + rows] = rows_buf[pl.ds(f, rows, faces), :]
     trace_wide = wide(pads[3], deep)
-    loads[2].wait()
-    loads[3].wait()
-    for load in loads[4:]:
-        load.start()
+    trace[quants * rows :, :] = jnp.zeros((trace.shape[0] - quants * rows, flat), F32)
+    first[2].wait()
+    for group in triples[:-1]:
+        multiply(stiff_wide, lambda q: dofs_ref[q], keep_z(0), group)
+    first[3].wait()
     factor = DT_STEP
     for degree in range(1, DERIVS):
-        if degree == 1:
-            multiply(stiff_wide, lambda q: dofs_ref[q], keep_z)
-        else:
-            multiply(stiff_wide, lambda q: x_buf[q], keep_z)
+        at, then = (degree - 1) % 2, degree % 2
         past = factor
         factor = factor * DT_STEP / (degree + 1)
-        for group in triples:
-            for q, fresh in zip(group, apply_star(group)):
-                if degree < DERIVS - 1:
+        last = degree == DERIVS - 1
+        for t, group in enumerate(triples):
+            if t == 0:
+                source = dofs_ref if degree == 1 else x_buf
+                multiply(stiff_wide, lambda q: source[q], keep_z(at), triples[-1])
+            elif last:
+                multiply(trace_wide, lambda q: integ[q], keep_trace, triples[t - 1])
+            else:
+                multiply(stiff_wide, lambda q: x_buf[q], keep_z(then), triples[t - 1])
+            for q, fresh in zip(group, apply_star(at, group)):
+                if not last:
                     x_buf[q] = fresh
                 base = past * dofs_ref[q] if degree == 1 else integ[q]
                 integ[q] = base + factor * fresh
-
-    for k in (4, 5, 6):
-        loads[k].wait()
-    trace[quants * rows :, :] = jnp.zeros((trace.shape[0] - quants * rows, flat), F32)
-
-    def keep_trace(q, result):
-        for f in range(faces):
-            first = f * face_rows
-            trace[q * rows : (q + 1) * rows, f * elems : (f + 1) * elems] = result[
-                first : first + rows
-            ]
-
-    multiply(trace_wide, lambda q: integ[q], keep_trace)
+            if 1 < degree and t < len(triples) - 1:
+                fence()
+    multiply(trace_wide, lambda q: integ[q], keep_trace, triples[-1])
     trace_split = stacked(trace[...])
 
-    def table(keys, wanted):
-        return jnp.where(keys == wanted, 1.0, 0.0).astype(BF16)
-
-    fault_keys = lax.broadcasted_iota(jnp.int32, (flat, slots), 0)
-    fault_table = table(fault_keys, faces_ref[...].reshape(1, slots))
+    def table(height, wanted, base=0):
+        keys = lax.broadcasted_iota(jnp.int16, (height, wanted.shape[1]), 0)
+        match = keys == (wanted - base).astype(jnp.int16)
+        return jnp.where(match, jnp.array(1.0, BF16), jnp.array(0.0, BF16))
+
+    arrived(4)
+    fault_table = table(flat, faces_ref[...].reshape(1, slots))
     own_trace = pick(trace_split, fault_table)
     orient = jnp.where(core == 0, 1.0, -1.0).astype(F32)
     for k in range(6):
@@ -269,28 +302,36 @@
         own_c[k, 0:points] = frame[k, 0:points] - orient * impedance * frame[k + 3, 0:points]
 
     pl.semaphore_wait(barrier, len(shifts) + chips)
-    to_partner = pltpu.make_async_remote_copy(
-        src_ref=own_c,
-        dst_ref=other_c,
-        send_sem=fault_send,
-        recv_sem=fault_recv,
-        device_id=partner,
-        device_id_type=MESH,
-    )
+    def across(first_row, last_row, n):
+        return pltpu.make_async_remote_copy(
+            src_ref=own_c.at[first_row:last_row],
+            dst_ref=other_c.at[first_row:last_row],
+            send_sem=fault_send.at[n],
+            recv_sem=fault_recv.at[n],
+            device_id=partner,
+            device_id_type=MESH,
+        )
+
+    to_partner = across(0, 2, 0)
+    dip_over = across(2, 3, 1)
     to_partner.start()
 
-    loads[7].wait()
+    arrived(5)
     small[0:blocks, 0:block] = send_ref[...]
     half_rows = trace.shape[0] // 2
-    doubled = small[...] + pltpu.roll(small[...], block, 1)
     lane = lax.broadcasted_iota(jnp.int32, (half_rows, LANES), 1)
-    block_keys = lax.broadcasted_iota(jnp.int32, (flat, blocks * LANES), 0)
-    wanted = jnp.concatenate([doubled[o : o + 1] for o in range(blocks)], axis=1)
-    chosen = pick(trace_split, table(block_keys, wanted))
+    near_half = lane < block
+    behind = pltpu.roll(small[...], block, 1)
+    duos = range(0, blocks, 2)
+    wanted = jnp.concatenate([small[o : o + 1] + behind[o + 1 : o + 2] for o in duos], axis=1)
+    chosen = pick_apart(trace_split, table(flat, wanted))
     copies = []
+    for o in duos:
+        part = chosen[:, o // 2 * LANES : (o // 2 + 1) * LANES]
+        upper, lower = part[:half_rows], part[half_rows:]
+        halo_out[o] = jnp.where(near_half, upper, pltpu.roll(lower, block, 1))
+        halo_out[o + 1] = jnp.where(near_half, pltpu.roll(upper, block, 1), lower)
     for o, shift in enumerate(shifts):
-        part = chosen[:, o * LANES : (o + 1) * LANES]
-        halo_out[o] = jnp.where(lane < block, part[:half_rows], part[half_rows:])
         copies.append(
             pltpu.make_async_remote_copy(
                 src_ref=halo_out.at[o],
@@ -301,23 +342,24 @@
                 device_id_type=MESH,
             )
         )
-        copies[-1].start()
+    for o in (0, 2):
+        copies[o].start()
 
     turned = [jnp.transpose(pads[d])[0:deep] for d in range(3)]
     turned_wide = wide(jnp.concatenate(turned, axis=0), deep)
-    multiply(turned_wide, lambda q: integ[q], keep_z)
     for group in triples:
-        for q, fresh in zip(group, apply_star(group)):
+        multiply(turned_wide, lambda q: integ[q], keep_z(0), group)
+    for group in triples:
+        for q, fresh in zip(group, apply_star(0, group)):
             out_ref[q] = dofs_ref[q] + fresh
-
-    loads[8].wait()
-    loads[12].wait()
+        fence()
+
+    arrived(12)
     to_partner.wait_recv()
     fric_a, state_value, normal_pre, shear_pre = (par_ref[k] for k in range(4))
     imp_p, imp_s = par_ref[5], par_ref[6]
     normal_hat = 0.5 * (own_c[0, 0:points] + other_c[0, 0:points])
     locked = shear_pre + 0.5 * (own_c[1, 0:points] + other_c[1, 0:points])
-    dip_hat = 0.5 * (own_c[2, 0:points] + other_c[2, 0:points])
     effective = jnp.maximum(normal_pre - normal_hat, 0.0)
     growth = 0.5 * jnp.exp(state_value / fric_a)
     strength = effective * fric_a
@@ -349,8 +391,13 @@
         ).start()
 
     each_hop(send_bound)
-
-    loads[9].wait()
+    for o in (1, 3):
+        copies[o].start()
+    dip_over.start()
+
+    arrived(13)
+    dip_over.wait_recv()
+    dip_hat = 0.5 * (own_c[2, 0:points] + other_c[2, 0:points])
     hats = [normal_hat, shear_hat, dip_hat]
     for k in range(3):
         impedance = imp_p if k == 0 else imp_s
@@ -371,50 +418,98 @@
     half = spread.shape[0] // 2
     lifted[...] = spread[:half] + spread[half:]
 
-    loads[10].wait()
-    loads[11].wait()
+    arrived(len(later))
     neighbour = jnp.concatenate([neigh_ref[f : f + 1, :] for f in range(faces)], axis=1)
-    face_keys = lax.broadcasted_iota(jnp.int32, (flat, flat), 0)
-    local_part = pick(trace_split, table(face_keys, neighbour))
-    place = lax.broadcasted_iota(jnp.int32, (blocks * LANES, flat), 0)
-    spot = lax.rem(place, LANES)
-    slot_key = flat + place // LANES * block
-    top_table = table(jnp.where(spot < block, slot_key + spot, -1), neighbour)
-    low_table = table(jnp.where(spot < block, -1, slot_key + spot - block), neighbour)
-
-    for copy in copies:
-        copy.wait_recv()
-    arrived = stacked(jnp.concatenate([halo_in[o] for o in range(blocks)], axis=1))
-    outer = local_part + jnp.concatenate(
-        [pick(arrived, top_table), pick(arrived, low_table)], axis=0
-    )
+    local_part = pick(trace_split, table(flat, neighbour))
+    lane_tile = lax.broadcasted_iota(jnp.int32, (faces, LANES), 1)
+    wide_lane = lax.broadcasted_iota(jnp.int32, (basis, LANES), 1)
+    duo_faces = range(0, faces, 2)
+
+    def face_pairs(tile):
+        shifted = pltpu.roll(jnp.concatenate([tile[1:], tile[:1]], axis=0), EDGE, 1)
+        return jnp.where(lane_tile < EDGE, tile, shifted)
+
+    paired = face_pairs(neigh_ref[...])
+    far_keys = jnp.concatenate([paired[f : f + 1] for f in duo_faces], axis=1)
+    far_table = table(blocks * block, far_keys, flat)
+    for q in range(quants):
+        for j in range(quants):
+            pair_flux[q, j] = face_pairs(flux_ref[1, q, j])
     lift_pair = stacked(jnp.transpose(pads[3])[:deep])
-    pieces = []
+    lift_wide = jnp.concatenate([lift_pair[:deep], lift_pair[deep:], lift_pair[:deep]], axis=1)
     for f in range(faces):
         columns = slice(f * elems, (f + 1) * elems)
-        values = []
         for q in range(quants):
             summed = lifted[q * rows : (q + 1) * rows, columns]
             for j in range(quants):
                 inner = trace[j * rows : (j + 1) * rows, columns]
-                near = outer[j * rows : (j + 1) * rows, columns]
+                near = local_part[j * rows : (j + 1) * rows, columns]
                 summed = summed + flux_ref[0, q, j, f : f + 1, :] * inner
                 summed = summed + flux_ref[1, q, j, f : f + 1, :] * near
-            values.append(summed)
-        pieces.append(values)
+            vals[q, f * face_rows : f * face_rows + rows] = summed
+
+    def three(joined):
+        high, low = split(joined)
+        return jnp.concatenate([high, high, low], axis=0)
+
+    for group in triples:
+        result = dot(lift_wide, three(jnp.concatenate([vals[q] for q in group], axis=1)))
+        for n, q in enumerate(group):
+            out_ref[q] = out_ref[q] - result[:basis, n * elems : (n + 1) * elems]
+
+    sorted_rows = jnp.concatenate(
+        [pads[3, f * face_rows : (f + 1) * face_rows] for f in (*duo_faces, *range(1, faces, 2))],
+        axis=0,
+    )
+    tall_lift = jnp.transpose(sorted_rows)[:deep]
+    lift_lane = lax.broadcasted_iota(jnp.int32, (deep, LANES), 1)
+    both_lifts = jnp.concatenate(
+        [
+            jnp.where(lift_lane < deep, tall_lift, 0.0),
+            jnp.where(lift_lane < deep, pltpu.roll(tall_lift, LANES - deep, 1), 0.0),
+        ],
+        axis=0,
+    )
+    far_wide = wide(both_lifts, deep)
+
+    for copy in copies:
+        copy.wait_recv()
+    columns = []
+    for o in duos:
+        upper, lower = halo_in[o], halo_in[o + 1]
+        columns.append(
+            jnp.concatenate(
+                [
+                    jnp.where(near_half, upper, pltpu.roll(lower, block, 1)),
+                    jnp.where(near_half, pltpu.roll(upper, block, 1), lower),
+                ],
+                axis=0,
+            )
+        )
+    far = pick(stacked(jnp.concatenate(columns, axis=1)), far_table)
     rest = jnp.zeros((face_rows - rows, LANES), F32)
-    for group in pairs:
-        columns = [
-            jnp.concatenate(
-                [part for f in range(faces) for part in (pieces[f][q], rest)], axis=0
-            )
-            for q in group
-        ]
-        result = product(lift_pair, jnp.concatenate(columns, axis=1))[:basis]
+    for group in triples:
+        parts = []
+        for q in group:
+            pieces = []
+            for c in range(len(duo_faces)):
+                summed = None
+                for j in range(quants):
+                    term = pair_flux[q, j, 2 * c : 2 * c + 1, :] * far[
+                        j * rows : (j + 1) * rows, c * LANES : (c + 1) * LANES
+                    ]
+                    summed = term if summed is None else summed + term
+                pieces += [summed, rest]
+            parts.append(jnp.concatenate(pieces, axis=0))
+        result = dot(far_wide, three(jnp.concatenate(parts, axis=1)))
         for n, q in enumerate(group):
-            out_ref[q] = out_ref[q] - result[:, n * elems : (n + 1) * elems]
+            even = result[:basis, n * elems : (n + 1) * elems]
+            odd = result[deep : deep + basis, n * elems : (n + 1) * elems]
+            both = even + pltpu.roll(odd, LANES - EDGE, 1)
+            out_ref[q] = out_ref[q] - jnp.where(wide_lane < EDGE, both, 0.0)
 
     to_partner.wait_send()
+    dip_over.wait_send()
     for copy in copies:
         copy.wait_send()
     best = bound_out[...]
@@ -493,9 +588,9 @@
             scratch_shapes=[
                 *(pltpu.VMEM(array.shape, array.dtype) for array in loaded),
                 pltpu.SMEM(fault_count.shape, fault_count.dtype),
-                pltpu.SemaphoreType.DMA((len(loaded) + 1,)),
+                pltpu.SemaphoreType.DMA((len(loaded) + fault_params.shape[0] + 1,)),
                 pltpu.VMEM((quants, basis, elems), F32),
-                pltpu.VMEM((3, quants, basis, elems), F32),
+                pltpu.VMEM((2, 3, quants, basis, elems), F32),
                 pltpu.VMEM((quants, basis, elems), F32),
                 pltpu.VMEM((trace_rows, faces * elems), F32),
                 pltpu.VMEM((4, LANES, LANES), F32),
@@ -508,12 +603,14 @@
                 pltpu.VMEM((blocks, trace_rows // 2, LANES), F32),
                 pltpu.VMEM((trace_rows, faces * elems), F32),
                 pltpu.VMEM((trace_rows, slots), F32),
+                pltpu.VMEM((quants, LANES, elems), F32),
+                pltpu.VMEM((quants, quants, faces, elems), F32),
                 pltpu.VMEM((1, LANES), F32),
                 pltpu.VMEM((hops, 1, LANES), F32),
                 pltpu.SemaphoreType.DMA((blocks,)),
                 pltpu.SemaphoreType.DMA((blocks,)),
-                pltpu.SemaphoreType.DMA,
-                pltpu.SemaphoreType.DMA,
+                pltpu.SemaphoreType.DMA((2,)),
+                pltpu.SemaphoreType.DMA((2,)),
                 pltpu.SemaphoreType.DMA,
                 pltpu.SemaphoreType.DMA,
             ],

time: 18.9 us -> 18 us (0.952)
  Pallas kernels: 17.4 us -> 16.6 us
    pallas_call x1, Pallas kernels: 16.7 us -> 15.9 us  [on_device(): pl.pallas_call(functools.partial(kernel, chips, cores), out_shape=(pltpu....]
where the time goes in v2:
time: 18 us; the launch traced here: 17.9 us
  Pallas kernels  16.6 us (92%)
  between operations  1.29 us (7%)
    pallas_call x1, Pallas kernels, on_device(): pl.pallas_call(functools.partial(kernel, chips, cores), out_shape=(pltpu....  15.9 us
    pallas_call x1, Pallas kernels, on_device(): pl.pallas_call(store, out_shape=(jax.ShapeDtypeStruct(new_dofs.shape, F32...  0.73 us

profile of v2, /device:TPU:0, one launch (start us, length us, event | category | flops | bytes accessed | tf_op | source)
XLA Modules:
  0.0 17.9 jit_solution(8543929769902620745)
XLA Ops:
  1.3 15.9 %shard_map.148 = (f32[9,56,128]{2,1,0:T(8,128)S(1)}, f32[21,384]{1,0:T(8,128)S(1)}, f32[8,128]{1,0:T(8,128)S(1)}) custom-call(f32[9,56,128]{2,1,0:T(8,128)} %dofs_hbm.1, f32[9,9,3,128]{3,2,1,0:T(4,128)} %bitcast.6, f32[3,56,56]{2,1,0:T(8,128)} %stiff_hbm.1, f32[21,4,56]{2,1,0:T(4,128)} %bitcast.8, f32[2,9,9,4,128]{4,3,2,1,0:T(4,128)} %bitcast.5, ...), custom_call_target="tpu_custom_call" | custom-call | tf_op jit(solution)/shard_map/pallas_call | solution.py:579
  17.1 0.7 %shard_map.149 = (f32[9,56,128]{2,1,0:T(8,128)}, f32[21,384]{1,0:T(8,128)}, f32[1,1]{1,0:T(1,128)}) custom-call(f32[9,56,128]{2,1,0:T(8,128)S(1)} %get-tuple-element.9.dofs, f32[21,384]{1,0:T(8,128)S(1)} %get-tuple-element.10.slip, f32[8,128]{1,0:T(8,128)S(1)} %get-tuple-element.11.step), custom_call_target="tpu_custom_call" | custom-call | tf_op jit(solution)/shard_map/pallas_call | solution.py:636

commit v3 on v2

--- a/solution.py
+++ b/solution.py
@@ -43,11 +43,6 @@
     half = pair.shape[0] // 2
     both = dot(pair, table)
     return both[:half] + both[half:]
-
-
-def pick_apart(pair, table):
-    half = pair.shape[0] // 2
-    return dot(pair[:half], table) + dot(pair[half:], table)
 
 
 def wide(matrix, width):
@@ -98,6 +93,14 @@
     small,
     own_c,
     other_c,
+    own_dip,
+    other_dip,
+    own_trace,
+    chosen,
+    local_part,
+    trace_parts,
+    fault_table,
+    send_table,
     frame,
     halo_out,
     halo_in,
@@ -156,9 +159,9 @@
         load(source, target)
         for source, target in (
             (faces_hbm, faces_ref),
+            (send_hbm, send_ref),
             (rot_hbm, rot_ref),
             *((par_hbm.at[k], par_ref.at[k]) for k in (5, 6)),
-            (send_hbm, send_ref),
             *((par_hbm.at[k], par_ref.at[k]) for k in range(5)),
             (guess_hbm, guess_ref),
             (count_hbm, count_ref),
@@ -168,7 +171,7 @@
             (flux_hbm.at[1], flux_ref.at[1]),
         )
     ]
-    for copy in first:
+    for copy in first + later:
         copy.start()
     waiting = list(later)
 
@@ -201,9 +204,8 @@
     rows_buf[...] = jnp.zeros(rows_buf.shape, F32)
     small[...] = jnp.zeros(small.shape, jnp.int32)
     vals[...] = jnp.zeros(vals.shape, F32)
+    chosen[quants * rows :, :] = jnp.zeros((chosen.shape[0] - quants * rows, chosen.shape[1]), F32)
     first[0].wait()
-    for copy in later:
-        copy.start()
     for d in range(3):
         pads[d, 0:basis, 0:basis] = stiff_ref[d]
     stiff_wide = wide(-jnp.concatenate([pads[d, 0:deep] for d in range(3)], axis=0), deep)
@@ -258,18 +260,62 @@
     for group in triples[:-1]:
         multiply(stiff_wide, lambda q: dofs_ref[q], keep_z(0), group)
     first[3].wait()
+
+    def table(height, wanted, base=0):
+        keys = lax.broadcasted_iota(jnp.int16, (height, wanted.shape[1]), 0)
+        match = keys == (wanted - base).astype(jnp.int16)
+        return jnp.where(match, jnp.array(1.0, BF16), jnp.array(0.0, BF16))
+
+    duos = range(0, blocks, 2)
+
+    def build_tables():
+        arrived(2)
+        fault_table[...] = table(flat, faces_ref[...].reshape(1, slots))
+        small[0:blocks, 0:block] = send_ref[...]
+        behind = pltpu.roll(small[...], block, 1)
+        wanted = jnp.concatenate(
+            [small[o : o + 1] + behind[o + 1 : o + 2] for o in duos], axis=1
+        )
+        send_table[...] = table(flat, wanted)
+
+    tier = trace_parts.shape[0] // (2 * len(triples))
+
+    def split_trace(g):
+        height = len(triples[g]) * rows
+        base = triples[g][0] * rows
+        spare = jnp.zeros((tier - height, flat), F32)
+        both = stacked(jnp.concatenate([trace[base : base + height, :], spare], axis=0))
+        trace_parts[2 * g * tier : 2 * (g + 1) * tier] = both
+
+    def place(both, g, target):
+        height = len(triples[g]) * rows
+        base = triples[g][0] * rows
+        target[base : base + height, :] = both[:height] + both[tier : tier + height]
+
+    def pick_group(g, chosen_table, target):
+        place(dot(trace_parts[2 * g * tier : 2 * (g + 1) * tier], chosen_table), g, target)
+
+    def pick_all(chosen_table, target):
+        both = dot(trace_parts[...], chosen_table)
+        for g in range(len(triples)):
+            place(both[2 * g * tier : 2 * (g + 1) * tier], g, target)
+
     factor = DT_STEP
     for degree in range(1, DERIVS):
         at, then = (degree - 1) % 2, degree % 2
         past = factor
         factor = factor * DT_STEP / (degree + 1)
         last = degree == DERIVS - 1
+        if last:
+            build_tables()
         for t, group in enumerate(triples):
             if t == 0:
                 source = dofs_ref if degree == 1 else x_buf
                 multiply(stiff_wide, lambda q: source[q], keep_z(at), triples[-1])
             elif last:
                 multiply(trace_wide, lambda q: integ[q], keep_trace, triples[t - 1])
+                if t > 1:
+                    split_trace(t - 2)
             else:
                 multiply(stiff_wide, lambda q: x_buf[q], keep_z(then), triples[t - 1])
             for q, fresh in zip(group, apply_star(at, group)):
@@ -277,58 +323,63 @@
                     x_buf[q] = fresh
                 base = past * dofs_ref[q] if degree == 1 else integ[q]
                 integ[q] = base + factor * fresh
-            if 1 < degree and t < len(triples) - 1:
+            if t < len(triples) - 1:
                 fence()
     multiply(trace_wide, lambda q: integ[q], keep_trace, triples[-1])
-    trace_split = stacked(trace[...])
-
-    def table(height, wanted, base=0):
-        keys = lax.broadcasted_iota(jnp.int16, (height, wanted.shape[1]), 0)
-        match = keys == (wanted - base).astype(jnp.int16)
-        return jnp.where(match, jnp.array(1.0, BF16), jnp.array(0.0, BF16))
-
-    arrived(4)
-    fault_table = table(flat, faces_ref[...].reshape(1, slots))
-    own_trace = pick(trace_split, fault_table)
+    split_trace(len(triples) - 2)
+    split_trace(len(triples) - 1)
+    pick_all(fault_table[...], own_trace)
     orient = jnp.where(core == 0, 1.0, -1.0).astype(F32)
-    for k in range(6):
+    chunks = [slice(c * LANES, (c + 1) * LANES) for c in range(slots // LANES)]
+    arrived(5)
+
+    def turn(k, lanes):
         summed = None
         for j in range(quants):
-            term = rot_ref[j, k : k + 1, :] * own_trace[j * rows : (j + 1) * rows]
+            term = rot_ref[j, k : k + 1, lanes] * own_trace[j * rows : (j + 1) * rows, lanes]
             summed = term if summed is None else summed + term
-        frame[k] = summed
-    for k in range(3):
-        impedance = par_ref[5 if k == 0 else 6]
-        own_c[k, 0:points] = frame[k, 0:points] - orient * impedance * frame[k + 3, 0:points]
-
-    pl.semaphore_wait(barrier, len(shifts) + chips)
-    def across(first_row, last_row, n):
+        frame[k, :, lanes] = summed
+        return summed[:points]
+
+    def face_both(k, lanes):
+        impedance = par_ref[5 if k == 0 else 6, :, lanes]
+        stress, speed = turn(k, lanes), turn(k + 3, lanes)
+        return stress - orient * impedance * speed
+
+    def across(c):
         return pltpu.make_async_remote_copy(
-            src_ref=own_c.at[first_row:last_row],
-            dst_ref=other_c.at[first_row:last_row],
-            send_sem=fault_send.at[n],
-            recv_sem=fault_recv.at[n],
+            src_ref=own_c.at[c],
+            dst_ref=other_c.at[c],
+            send_sem=fault_send.at[c],
+            recv_sem=fault_recv.at[c],
             device_id=partner,
             device_id_type=MESH,
         )
 
-    to_partner = across(0, 2, 0)
-    dip_over = across(2, 3, 1)
-    to_partner.start()
-
-    arrived(5)
-    small[0:blocks, 0:block] = send_ref[...]
+    crossing = [across(c) for c in range(len(chunks))]
+    dip_over = pltpu.make_async_remote_copy(
+        src_ref=own_dip,
+        dst_ref=other_dip,
+        send_sem=fault_send.at[len(chunks)],
+        recv_sem=fault_recv.at[len(chunks)],
+        device_id=partner,
+        device_id_type=MESH,
+    )
+    for c, lanes in enumerate(chunks):
+        for k in range(2):
+            own_c[c, k] = face_both(k, lanes)
+        if c == 0:
+            pl.semaphore_wait(barrier, len(shifts) + chips)
+        crossing[c].start()
+
+    pick_all(send_table[...], chosen)
     half_rows = trace.shape[0] // 2
     lane = lax.broadcasted_iota(jnp.int32, (half_rows, LANES), 1)
     near_half = lane < block
-    behind = pltpu.roll(small[...], block, 1)
-    duos = range(0, blocks, 2)
-    wanted = jnp.concatenate([small[o : o + 1] + behind[o + 1 : o + 2] for o in duos], axis=1)
-    chosen = pick_apart(trace_split, table(flat, wanted))
     copies = []
     for o in duos:
-        part = chosen[:, o // 2 * LANES : (o // 2 + 1) * LANES]
-        upper, lower = part[:half_rows], part[half_rows:]
+        lanes = slice(o // 2 * LANES, (o // 2 + 1) * LANES)
+        upper, lower = chosen[:half_rows, lanes], chosen[half_rows:, lanes]
         halo_out[o] = jnp.where(near_half, upper, pltpu.roll(lower, block, 1))
         halo_out[o + 1] = jnp.where(near_half, pltpu.roll(upper, block, 1), lower)
     for o, shift in enumerate(shifts):
@@ -342,42 +393,46 @@
                 device_id_type=MESH,
             )
         )
-    for o in (0, 2):
-        copies[o].start()
-
-    turned = [jnp.transpose(pads[d])[0:deep] for d in range(3)]
-    turned_wide = wide(jnp.concatenate(turned, axis=0), deep)
-    for group in triples:
-        multiply(turned_wide, lambda q: integ[q], keep_z(0), group)
-    for group in triples:
-        for q, fresh in zip(group, apply_star(0, group)):
-            out_ref[q] = dofs_ref[q] + fresh
-        fence()
+    urgent = [lax.rem(me + shift + total, total) < cores for shift in shifts]
+
+    def start_if(wanted):
+        for copy, first_of_all in zip(copies, urgent):
+            pl.when(first_of_all == wanted)(copy.start)
+
+    start_if(True)
+    for lanes in chunks:
+        own_dip[:, lanes] = face_both(2, lanes)
 
     arrived(12)
-    to_partner.wait_recv()
-    fric_a, state_value, normal_pre, shear_pre = (par_ref[k] for k in range(4))
-    imp_p, imp_s = par_ref[5], par_ref[6]
-    normal_hat = 0.5 * (own_c[0, 0:points] + other_c[0, 0:points])
-    locked = shear_pre + 0.5 * (own_c[1, 0:points] + other_c[1, 0:points])
-    effective = jnp.maximum(normal_pre - normal_hat, 0.0)
-    growth = 0.5 * jnp.exp(state_value / fric_a)
-    strength = effective * fric_a
-    slip_speed = guess_ref[...]
-    for _ in range(NEWTON):
-        scaled = slip_speed * growth
-        magnitude = jnp.abs(scaled)
-        root = jnp.sqrt(1.0 + scaled * scaled)
-        logged = jnp.log(magnitude + root)
-        logged = jnp.where(scaled < 0.0, -logged, logged)
-        mismatch = locked - 0.5 * imp_s * slip_speed - strength * logged
-        slope_value = -0.5 * imp_s - strength * growth / root
-        slip_speed = slip_speed - mismatch / slope_value
-    shear_hat = locked - shear_pre - 0.5 * imp_s * slip_speed
-    live = lax.broadcasted_iota(jnp.int32, (points, slots), 1) < count_ref[0]
-    slip_ref[...] = jnp.where(live, slip_speed, 0.0)
-    bound = jnp.where(live, par_ref[4] / (jnp.abs(slip_speed) + 1.0), FAR_BOUND)
-    bound = jnp.min(jnp.min(bound, axis=0, keepdims=True), axis=1, keepdims=True)
+    least = None
+    faced = []
+    for c, lanes in enumerate(chunks):
+        crossing[c].wait_recv()
+        fric_a, state_value, normal_pre, shear_pre = (par_ref[k, :, lanes] for k in range(4))
+        imp_s = par_ref[6, :, lanes]
+        normal_hat = 0.5 * (own_c[c, 0] + other_c[c, 0])
+        locked = shear_pre + 0.5 * (own_c[c, 1] + other_c[c, 1])
+        effective = jnp.maximum(normal_pre - normal_hat, 0.0)
+        growth = 0.5 * jnp.exp(state_value / fric_a)
+        strength = effective * fric_a
+        slip_speed = guess_ref[:, lanes]
+        for _ in range(NEWTON):
+            scaled = slip_speed * growth
+            magnitude = jnp.abs(scaled)
+            root = jnp.sqrt(1.0 + scaled * scaled)
+            logged = jnp.log(magnitude + root)
+            logged = jnp.where(scaled < 0.0, -logged, logged)
+            mismatch = locked - 0.5 * imp_s * slip_speed - strength * logged
+            slope_value = -0.5 * imp_s - strength * growth / root
+            slip_speed = slip_speed - mismatch / slope_value
+        shear_hat = locked - shear_pre - 0.5 * imp_s * slip_speed
+        slot = lax.broadcasted_iota(jnp.int32, (points, LANES), 1) + c * LANES
+        live = slot < count_ref[0]
+        slip_ref[:, lanes] = jnp.where(live, slip_speed, 0.0)
+        bound = jnp.where(live, par_ref[4, :, lanes] / (jnp.abs(slip_speed) + 1.0), FAR_BOUND)
+        least = bound if least is None else jnp.minimum(least, bound)
+        faced.append((normal_hat, shear_hat, live))
+    bound = jnp.min(jnp.min(least, axis=0, keepdims=True), axis=1, keepdims=True)
     bound_out[...] = jnp.broadcast_to(bound, (1, LANES))
 
     def send_bound(hop):
@@ -391,36 +446,44 @@
         ).start()
 
     each_hop(send_bound)
-    for o in (1, 3):
-        copies[o].start()
     dip_over.start()
+    start_if(False)
+    turned = [jnp.transpose(pads[d])[0:deep] for d in range(3)]
+    turned_wide = wide(jnp.concatenate(turned, axis=0), deep)
+    for group in triples:
+        multiply(turned_wide, lambda q: integ[q], keep_z(0), group)
+    for group in triples:
+        for q, fresh in zip(group, apply_star(0, group)):
+            out_ref[q] = dofs_ref[q] + fresh
+        fence()
+
 
     arrived(13)
     dip_over.wait_recv()
-    dip_hat = 0.5 * (own_c[2, 0:points] + other_c[2, 0:points])
-    hats = [normal_hat, shear_hat, dip_hat]
-    for k in range(3):
-        impedance = imp_p if k == 0 else imp_s
-        hats.append(
-            frame[k + 3, 0:points] + orient * (hats[k] - frame[k, 0:points]) / impedance
-        )
     fvals[...] = jnp.zeros(fvals.shape, F32)
-    for q in range(quants):
-        summed = None
-        for k in range(6):
-            term = fflux_ref[q, k : k + 1, :] * hats[k]
-            summed = term if summed is None else summed + term
-        fvals[q * rows : q * rows + points, :] = jnp.where(live, summed, 0.0)
+    for lanes, (normal_hat, shear_hat, live) in zip(chunks, faced):
+        hats = [normal_hat, shear_hat, 0.5 * (own_dip[:, lanes] + other_dip[:, lanes])]
+        for k in range(3):
+            impedance = par_ref[5 if k == 0 else 6, :, lanes]
+            past = frame[k, 0:points, lanes]
+            hats.append(frame[k + 3, 0:points, lanes] + orient * (hats[k] - past) / impedance)
+        for q in range(quants):
+            summed = None
+            for k in range(6):
+                term = fflux_ref[q, k : k + 1, lanes] * hats[k]
+                summed = term if summed is None else summed + term
+            fvals[q * rows : q * rows + points, lanes] = jnp.where(live, summed, 0.0)
     spread_pair = stacked(fvals[...])
     spread = lax.dot_general(
-        spread_pair, fault_table, (((1,), (1,)), ((), ())), preferred_element_type=F32
+        spread_pair, fault_table[...], (((1,), (1,)), ((), ())), preferred_element_type=F32
     )
     half = spread.shape[0] // 2
     lifted[...] = spread[:half] + spread[half:]
 
     arrived(len(later))
     neighbour = jnp.concatenate([neigh_ref[f : f + 1, :] for f in range(faces)], axis=1)
-    local_part = pick(trace_split, table(flat, neighbour))
+    near_table = table(flat, neighbour)
+    pick_all(near_table, local_part)
     lane_tile = lax.broadcasted_iota(jnp.int32, (faces, LANES), 1)
     wide_lane = lax.broadcasted_iota(jnp.int32, (basis, LANES), 1)
     duo_faces = range(0, faces, 2)
@@ -508,7 +571,8 @@
             both = even + pltpu.roll(odd, LANES - EDGE, 1)
             out_ref[q] = out_ref[q] - jnp.where(wide_lane < EDGE, both, 0.0)
 
-    to_partner.wait_send()
+    for copy in crossing:
+        copy.wait_send()
     dip_over.wait_send()
     for copy in copies:
         copy.wait_send()
@@ -596,8 +660,16 @@
                 pltpu.VMEM((4, LANES, LANES), F32),
                 pltpu.VMEM((up(rows * faces, 8), LANES), F32),
                 pltpu.VMEM((up(blocks, 8), LANES), jnp.int32),
-                pltpu.VMEM((3, points, slots), F32),
-                pltpu.VMEM((3, points, slots), F32),
+                pltpu.VMEM((slots // LANES, 2, points, LANES), F32),
+                pltpu.VMEM((slots // LANES, 2, points, LANES), F32),
+                pltpu.VMEM((points, slots), F32),
+                pltpu.VMEM((points, slots), F32),
+                pltpu.VMEM((trace_rows, slots), F32),
+                pltpu.VMEM((trace_rows, blocks // 2 * LANES), F32),
+                pltpu.VMEM((trace_rows, faces * elems), F32),
+                pltpu.VMEM((2 * (up(quants, 3) // 3) * up(3 * rows, 16), faces * elems), BF16),
+                pltpu.VMEM((faces * elems, slots), BF16),
+                pltpu.VMEM((faces * elems, blocks // 2 * LANES), BF16),
                 pltpu.VMEM((6, rows, slots), F32),
                 pltpu.VMEM((blocks, trace_rows // 2, LANES), F32),
                 pltpu.VMEM((blocks, trace_rows // 2, LANES), F32),
@@ -609,8 +681,8 @@
                 pltpu.VMEM((hops, 1, LANES), F32),
                 pltpu.SemaphoreType.DMA((blocks,)),
                 pltpu.SemaphoreType.DMA((blocks,)),
-                pltpu.SemaphoreType.DMA((2,)),
-                pltpu.SemaphoreType.DMA((2,)),
+                pltpu.SemaphoreType.DMA((slots // LANES + 1,)),
+                pltpu.SemaphoreType.DMA((slots // LANES + 1,)),
                 pltpu.SemaphoreType.DMA,
                 pltpu.SemaphoreType.DMA,
             ],

time: 18 us -> 17.5 us (0.972)
  Pallas kernels: 16.6 us -> 16 us
    pallas_call x1, Pallas kernels: 15.9 us -> 15.3 us  [on_device(): pl.pallas_call(functools.partial(kernel, chips, cores), out_shape=(pltpu....]
where the time goes in v3:
time: 17.5 us; the launch traced here: 17.3 us
  Pallas kernels  16 us (91%)
  between operations  1.29 us (7%)
    pallas_call x1, Pallas kernels, on_device(): pl.pallas_call(functools.partial(kernel, chips, cores), out_shape=(pltpu....  15.3 us
    pallas_call x1, Pallas kernels, on_device(): pl.pallas_call(store, out_shape=(jax.ShapeDtypeStruct(new_dofs.shape, F32...  0.73 us

profile of v3, /device:TPU:0, one launch (start us, length us, event | category | flops | bytes accessed | tf_op | source)
XLA Modules:
  0.0 17.3 jit_solution(11377729899316417346)
XLA Ops:
  1.3 15.3 %shard_map.148 = (f32[9,56,128]{2,1,0:T(8,128)S(1)}, f32[21,384]{1,0:T(8,128)S(1)}, f32[8,128]{1,0:T(8,128)S(1)}) custom-call(f32[9,56,128]{2,1,0:T(8,128)} %dofs_hbm.1, f32[9,9,3,128]{3,2,1,0:T(4,128)} %bitcast.6, f32[3,56,56]{2,1,0:T(8,128)} %stiff_hbm.1, f32[21,4,56]{2,1,0:T(4,128)} %bitcast.8, f32[2,9,9,4,128]{4,3,2,1,0:T(4,128)} %bitcast.5, ...), custom_call_target="tpu_custom_call" | custom-call | tf_op jit(solution)/shard_map/pallas_call | solution.py:643
  16.6 0.7 %shard_map.149 = (f32[9,56,128]{2,1,0:T(8,128)}, f32[21,384]{1,0:T(8,128)}, f32[1,1]{1,0:T(1,128)}) custom-call(f32[9,56,128]{2,1,0:T(8,128)S(1)} %get-tuple-element.9.dofs, f32[21,384]{1,0:T(8,128)S(1)} %get-tuple-element.10.slip, f32[8,128]{1,0:T(8,128)S(1)} %get-tuple-element.11.step), custom_call_target="tpu_custom_call" | custom-call | tf_op jit(solution)/shard_map/pallas_call | solution.py:708

commit v4 on v3

--- a/solution.py
+++ b/solution.py
@@ -249,17 +249,10 @@
                     sums[n] = term if sums[n] is None else sums[n] + term
         return sums
 
-    first[1].wait()
-    for p in range(points):
-        rows_buf[p * faces : (p + 1) * faces, 0:basis] = proj_ref[p]
-    for f in range(faces):
-        pads[3, f * face_rows : f * face_rows + rows] = rows_buf[pl.ds(f, rows, faces), :]
-    trace_wide = wide(pads[3], deep)
-    trace[quants * rows :, :] = jnp.zeros((trace.shape[0] - quants * rows, flat), F32)
     first[2].wait()
+    first[3].wait()
     for group in triples[:-1]:
         multiply(stiff_wide, lambda q: dofs_ref[q], keep_z(0), group)
-    first[3].wait()
 
     def table(height, wanted, base=0):
         keys = lax.broadcasted_iota(jnp.int16, (height, wanted.shape[1]), 0)
@@ -299,6 +292,14 @@
         both = dot(trace_parts[...], chosen_table)
         for g in range(len(triples)):
             place(both[2 * g * tier : 2 * (g + 1) * tier], g, target)
+
+    def trace_matrix():
+        first[1].wait()
+        for p in range(points):
+            rows_buf[p * faces : (p + 1) * faces, 0:basis] = proj_ref[p]
+        for f in range(faces):
+            pads[3, f * face_rows : f * face_rows + rows] = rows_buf[pl.ds(f, rows, faces), :]
+        return wide(pads[3], deep)
 
     factor = DT_STEP
     for degree in range(1, DERIVS):
@@ -308,6 +309,7 @@
         last = degree == DERIVS - 1
         if last:
             build_tables()
+            trace_wide = trace_matrix()
         for t, group in enumerate(triples):
             if t == 0:
                 source = dofs_ref if degree == 1 else x_buf
@@ -404,26 +406,34 @@
         own_dip[:, lanes] = face_both(2, lanes)
 
     arrived(12)
+
+    def slope_terms(slip_speed, growth):
+        scaled = slip_speed * growth
+        root = jnp.sqrt(1.0 + scaled * scaled)
+        logged = jnp.log(jnp.abs(scaled) + root)
+        return jnp.where(scaled < 0.0, -logged, logged), growth / root
+
+    ready = []
+    for lanes in chunks:
+        growth = 0.5 * jnp.exp(par_ref[1, :, lanes] / par_ref[0, :, lanes])
+        ready.append((growth, *slope_terms(guess_ref[:, lanes], growth)))
     least = None
     faced = []
     for c, lanes in enumerate(chunks):
         crossing[c].wait_recv()
-        fric_a, state_value, normal_pre, shear_pre = (par_ref[k, :, lanes] for k in range(4))
+        fric_a, normal_pre, shear_pre = (par_ref[k, :, lanes] for k in (0, 2, 3))
         imp_s = par_ref[6, :, lanes]
         normal_hat = 0.5 * (own_c[c, 0] + other_c[c, 0])
         locked = shear_pre + 0.5 * (own_c[c, 1] + other_c[c, 1])
         effective = jnp.maximum(normal_pre - normal_hat, 0.0)
-        growth = 0.5 * jnp.exp(state_value / fric_a)
         strength = effective * fric_a
         slip_speed = guess_ref[:, lanes]
-        for _ in range(NEWTON):
-            scaled = slip_speed * growth
-            magnitude = jnp.abs(scaled)
-            root = jnp.sqrt(1.0 + scaled * scaled)
-            logged = jnp.log(magnitude + root)
-            logged = jnp.where(scaled < 0.0, -logged, logged)
+        growth, logged, steepness = ready[c]
+        for repeat in range(NEWTON):
+            if repeat:
+                logged, steepness = slope_terms(slip_speed, growth)
             mismatch = locked - 0.5 * imp_s * slip_speed - strength * logged
-            slope_value = -0.5 * imp_s - strength * growth / root
+            slope_value = -0.5 * imp_s - strength * steepness
             slip_speed = slip_speed - mismatch / slope_value
         shear_hat = locked - shear_pre - 0.5 * imp_s * slip_speed
         slot = lax.broadcasted_iota(jnp.int32, (points, LANES), 1) + c * LANES

time: 17.5 us -> 17.4 us (level)
  no operation moved by 1% of the time
where the time goes in v4:
time: 17.4 us; the launch traced here: 17.2 us
  Pallas kernels  15.9 us (91%)
  between operations  1.29 us (7%)
    pallas_call x1, Pallas kernels, on_device(): pl.pallas_call(functools.partial(kernel, chips, cores), out_shape=(pltpu....  15.2 us
    pallas_call x1, Pallas kernels, on_device(): pl.pallas_call(store, out_shape=(jax.ShapeDtypeStruct(new_dofs.shape, F32...  0.73 us

profile of v4, /device:TPU:0, one launch (start us, length us, event | category | flops | bytes accessed | tf_op | source)
XLA Modules:
  0.0 17.2 jit_solution(7980953847752714643)
XLA Ops:
  1.3 15.2 %shard_map.148 = (f32[9,56,128]{2,1,0:T(8,128)S(1)}, f32[21,384]{1,0:T(8,128)S(1)}, f32[8,128]{1,0:T(8,128)S(1)}) custom-call(f32[9,56,128]{2,1,0:T(8,128)} %dofs_hbm.1, f32[9,9,3,128]{3,2,1,0:T(4,128)} %bitcast.6, f32[3,56,56]{2,1,0:T(8,128)} %stiff_hbm.1, f32[21,4,56]{2,1,0:T(4,128)} %bitcast.8, f32[2,9,9,4,128]{4,3,2,1,0:T(4,128)} %bitcast.5, ...), custom_call_target="tpu_custom_call" | custom-call | tf_op jit(solution)/shard_map/pallas_call | solution.py:653
  16.5 0.7 %shard_map.149 = (f32[9,56,128]{2,1,0:T(8,128)}, f32[21,384]{1,0:T(8,128)}, f32[1,1]{1,0:T(1,128)}) custom-call(f32[9,56,128]{2,1,0:T(8,128)S(1)} %get-tuple-element.9.dofs, f32[21,384]{1,0:T(8,128)S(1)} %get-tuple-element.10.slip, f32[8,128]{1,0:T(8,128)S(1)} %get-tuple-element.11.step), custom_call_target="tpu_custom_call" | custom-call | tf_op jit(solution)/shard_map/pallas_call | solution.py:718

commit v5 on v4

--- a/solution.py
+++ b/solution.py
@@ -325,7 +325,7 @@
                     x_buf[q] = fresh
                 base = past * dofs_ref[q] if degree == 1 else integ[q]
                 integ[q] = base + factor * fresh
-            if t < len(triples) - 1:
+            if t < len(triples) - 1 and not (last and t == 1):
                 fence()
     multiply(trace_wide, lambda q: integ[q], keep_trace, triples[-1])
     split_trace(len(triples) - 2)

time: 17.4 us -> 17.2 us (0.989)
  no operation moved by 1% of the time
where the time goes in v5:
time: 17.2 us; the launch traced here: 17.1 us
  Pallas kernels  15.8 us (92%)
  between operations  1.29 us (8%)
    pallas_call x1, Pallas kernels, on_device(): pl.pallas_call(functools.partial(kernel, chips, cores), out_shape=(pltpu....  15 us
    pallas_call x1, Pallas kernels, on_device(): pl.pallas_call(store, out_shape=(jax.ShapeDtypeStruct(new_dofs.shape, F32...  0.73 us

profile of v5, /device:TPU:0, one launch (start us, length us, event | category | flops | bytes accessed | tf_op | source)
XLA Modules:
  0.0 17.1 jit_solution(9269517574864364536)
XLA Ops:
  1.3 15.0 %shard_map.148 = (f32[9,56,128]{2,1,0:T(8,128)S(1)}, f32[21,384]{1,0:T(8,128)S(1)}, f32[8,128]{1,0:T(8,128)S(1)}) custom-call(f32[9,56,128]{2,1,0:T(8,128)} %dofs_hbm.1, f32[9,9,3,128]{3,2,1,0:T(4,128)} %bitcast.6, f32[3,56,56]{2,1,0:T(8,128)} %stiff_hbm.1, f32[21,4,56]{2,1,0:T(4,128)} %bitcast.8, f32[2,9,9,4,128]{4,3,2,1,0:T(4,128)} %bitcast.5, ...), custom_call_target="tpu_custom_call" | custom-call | tf_op jit(solution)/shard_map/pallas_call | solution.py:653
  16.3 0.7 %shard_map.149 = (f32[9,56,128]{2,1,0:T(8,128)}, f32[21,384]{1,0:T(8,128)}, f32[1,1]{1,0:T(1,128)}) custom-call(f32[9,56,128]{2,1,0:T(8,128)S(1)} %get-tuple-element.9.dofs, f32[21,384]{1,0:T(8,128)S(1)} %get-tuple-element.10.slip, f32[8,128]{1,0:T(8,128)S(1)} %get-tuple-element.11.step), custom_call_target="tpu_custom_call" | custom-call | tf_op jit(solution)/shard_map/pallas_call | solution.py:718
